TPU v7x, 32 devices: a whole 2x2x4 slice. The times are simulated.
32 devices in a mesh: gx: 2 (over x), gy: 4 (over z), gz: 4 (over y, core).
Axes of the slice: x: 2, y: 2, z: 4, core: 2. Of those that a mesh axis runs over, the one named last changes fastest.
Arguments:
- right_side: float32 [16, 64, 512], P('gx', 'gy', 'gz'), may hold values from -40 to 40
- fiber_class: int32 [16, 64, 512], P('gx', 'gy', 'gz'), may hold values from 0 to 15
- conductivity_scale: float32 [16, 64, 512], P('gx', 'gy', 'gz'), may hold values from 0.8 to 1.25
- class_tensor: float32 [6, 16], replicated, may hold values from -0.15 to 1.8, as said below
- block_ids: int32 [2, 4, 8], replicated, may hold values from 0 to 63, as said below
Outputs:
- solution: float32 [16, 64, 512], P('gx', 'gy', 'gz')
- residual: float32 [16, 64, 512], P('gx', 'gy', 'gz')
Inputs may be any that keep to these rules, and one draw needn't show every extreme that they name: `class_tensor`: column k is the tensor t I + (l - t) f f^T for a unit vector f, with 1 <= t <= 1.5 and 1.05 <= l / t <= 1.2. `block_ids`: each subdomain number names exactly 1 block.
All inputs are finite; a program needn't handle non-finite values.
Results may differ from a plain program's by a relative error of at most 0.0003.
Values sent between devices are 32-bit elements; how exact they have to be, the bound alone decides.
A program may use at most 64 MiB of HBM per device.

v0:
```python
import jax
import jax.numpy as jnp
from jax import lax
from jax.sharding import PartitionSpec as P

CX = 8
CY = 16
CZ = 128
ZBLK = 2
BZ = 64
COARSE = 64
NCLS = 16
ITERS = 2
STENCIL_TAPS = (
    (1, 0, 0, 0, 1.0),
    (-1, 0, 0, 0, 1.0),
    (0, 1, 0, 1, 1.0),
    (0, -1, 0, 1, 1.0),
    (0, 0, 1, 2, 1.0),
    (0, 0, -1, 2, 1.0),
    (1, 1, 0, 3, 0.5),
    (-1, -1, 0, 3, 0.5),
    (1, -1, 0, 3, -0.5),
    (-1, 1, 0, 3, -0.5),
    (1, 0, 1, 4, 0.5),
    (-1, 0, -1, 4, 0.5),
    (1, 0, -1, 4, -0.5),
    (-1, 0, 1, 4, -0.5),
    (0, 1, 1, 5, 0.5),
    (0, -1, -1, 5, 0.5),
    (0, 1, -1, 5, -0.5),
    (0, -1, 1, 5, -0.5),
)


def padded_2(cells, sides, width):
    for axis, dim in sides:
        count = lax.axis_size(axis)
        ends = count - 1
        head = lax.slice_in_dim(cells, 0, width, axis=dim)
        tail = lax.slice_in_dim(cells, cells.shape[dim] - width, cells.shape[dim], axis=dim)
        cells = jnp.concatenate(
            [
                lax.ppermute(tail, axis, [(i, (i + 1) % count) for i in range(ends)]),
                cells,
                lax.ppermute(head, axis, [((i + 1) % count, i) for i in range(ends)]),
            ],
            axis=dim,
        )
    return cells


def shifted(padded, step_x, step_y, step_z):
    width_x = padded.shape[-3] - 2
    width_y = padded.shape[-2] - 2
    width_z = padded.shape[-1] - 2
    return padded[
        1 + step_x : 1 + step_x + width_x,
        1 + step_y : 1 + step_y + width_y,
        1 + step_z : 1 + step_z + width_z,
    ]


def edge_weights(tensors, step_x, step_y, step_z, component, factor):
    layer = tensors[component]
    return 0.5 * factor * (shifted(layer, 0, 0, 0) + shifted(layer, step_x, step_y, step_z))


def operate(padded, tensors):
    centre = shifted(padded, 0, 0, 0)
    accumulated = jnp.zeros_like(centre)
    for step_x, step_y, step_z, component, factor in STENCIL_TAPS:
        weight = edge_weights(tensors, step_x, step_y, step_z, component, factor)
        accumulated = accumulated + weight * (centre - shifted(padded, step_x, step_y, step_z))
    return accumulated


def class_onehot(labels, count):
    return (labels[..., None] == jnp.arange(count, dtype=jnp.int32)).astype(jnp.float32)


def reach_onehot(length, offset):
    position = jnp.arange(length, dtype=jnp.int32)
    relative = (position + offset) // length + 1
    return (relative[:, None] == jnp.arange(3, dtype=jnp.int32)[None, :]).astype(jnp.float32)


def reach_blocks(length, offset, blocks):
    block_span = length // blocks
    position = jnp.arange(length, dtype=jnp.int32)
    owning = (position // block_span)[:, None] == jnp.arange(blocks, dtype=jnp.int32)[None, :]
    relative = ((position % block_span + offset) // block_span + 1)[:, None] == jnp.arange(
        3, dtype=jnp.int32
    )[None, :]
    return (owning[:, :, None] & relative[:, None, :]).astype(jnp.float32)


def centre_mask():
    places = jnp.arange(3, dtype=jnp.int32)
    return (
        (places[:, None, None] == 1) & (places[None, :, None] == 1) & (places[None, None, :] == 1)
    )


def build_tensors(matches, scale, class_tensor):
    return (
        jnp.stack(
            [
                jnp.sum(
                    jnp.where(matches, class_tensor[component][:, None, None, None], 0.0), axis=0
                )
                for component in range(6)
            ]
        )
        * scale[None]
    )


def body(right_side, fiber_class, conductivity_scale, class_tensor, block_ids):
    highest = lax.Precision.HIGHEST
    kinds = jnp.arange(NCLS, dtype=jnp.int32)
    matches = fiber_class[None] == kinds[:, None, None, None]
    local_tensor = build_tensors(matches, conductivity_scale, class_tensor)
    tensors = padded_2(local_tensor, (("gx", 1), ("gy", 2), ("gz", 3)), 1)
    place_x = lax.axis_index("gx")
    place_y = lax.axis_index("gy")
    place_z = lax.axis_index("gz")
    padded_ids = jnp.pad(block_ids, 1, constant_values=-1)
    window = lax.dynamic_slice(padded_ids, (place_x, place_y, place_z * ZBLK), (3, 3, ZBLK + 2))
    own_hot = class_onehot(window[1, 1, 1 : ZBLK + 1], COARSE)
    neighbours = jnp.stack([window[:, :, z_block : z_block + 3] for z_block in range(ZBLK)])
    rim_weight = jnp.zeros((ZBLK, 3, 3, 3), jnp.float32)
    for step_x, step_y, step_z, component, factor in STENCIL_TAPS:
        weight = edge_weights(tensors, step_x, step_y, step_z, component, factor)
        rim_weight = rim_weight + jnp.einsum(
            "xyz,xa,yb,zjc->jabc",
            weight,
            reach_onehot(CX, step_x),
            reach_onehot(CY, step_y),
            reach_blocks(CZ, step_z, ZBLK),
            precision=highest,
        )
    rim_weight = jnp.where(centre_mask()[None], 0.0, rim_weight)
    diagonal_terms = jnp.einsum(
        "jk,j->k", own_hot, jnp.sum(rim_weight, axis=(1, 2, 3)), precision=highest
    )
    coupling = jnp.einsum(
        "jk,jabc,jabcl->kl",
        own_hot,
        rim_weight,
        class_onehot(neighbours, COARSE),
        precision=highest,
    )
    coarse = lax.psum(jnp.diag(diagonal_terms) - coupling, ("gx", "gy", "gz"))
    coarse = 0.5 * (coarse + coarse.T)
    factor_lower = jnp.linalg.cholesky(coarse)

    def restrict(field):
        block_totals = jnp.sum(field.reshape(CX, CY, ZBLK, BZ), axis=(0, 1, 3))
        return jnp.einsum("jk,j->k", own_hot, block_totals, precision=highest)

    def prolong(coarse_values):
        values = jnp.einsum("jk,k->j", own_hot, coarse_values, precision=highest)
        return jnp.broadcast_to(values[None, None, :, None], (CX, CY, ZBLK, BZ)).reshape(CX, CY, CZ)

    def apply_field(field):
        padded = padded_2(field, (("gx", 0), ("gy", 1), ("gz", 2)), 1)
        return operate(padded, tensors)

    def coarse_solve(field):
        projected = lax.psum(restrict(field), ("gx", "gy", "gz"))
        return jax.scipy.linalg.cho_solve((factor_lower, True), projected)

    def deflation_image(coarse_values):
        result = apply_field(prolong(coarse_values))
        return result

    coarse_values = coarse_solve(right_side)
    coarse_part = prolong(coarse_values)
    residual = right_side - deflation_image(coarse_values)
    estimate = jnp.zeros_like(right_side)

    def joint_terms(field):
        product = apply_field(field)
        projected, norm_value, cross_value = lax.psum(
            (restrict(product), jnp.sum(field * field), jnp.sum(field * product)),
            ("gx", "gy", "gz"),
        )
        correction = jax.scipy.linalg.cho_solve((factor_lower, True), projected)
        image_field = product - deflation_image(correction)
        return (image_field, norm_value, cross_value - jnp.sum(projected * correction))

    image_field, norm_now, curvature_now = joint_terms(residual)
    step_size = norm_now / curvature_now
    direction = residual
    along = image_field
    for iteration in range(ITERS):
        estimate = estimate + step_size * direction
        residual = residual - step_size * along
        if iteration + 1 < ITERS:
            image_field, norm_next, curvature_now = joint_terms(residual)
            step_ratio = norm_next / norm_now
            step_size = norm_next / (curvature_now - step_ratio * norm_next / step_size)
            direction = residual + step_ratio * direction
            along = image_field + step_ratio * along
            norm_now = norm_next
    solution = coarse_part + estimate - prolong(coarse_solve(apply_field(estimate)))
    return (solution, residual)


def solution(mesh):
    placed = (P("gx", "gy", "gz"), P("gx", "gy", "gz"), P("gx", "gy", "gz"), P(), P())
    return jax.shard_map(
        body,
        mesh=mesh,
        in_specs=placed,
        out_specs=(P("gx", "gy", "gz"), P("gx", "gy", "gz")),
        check_vma=False,
    )
```

profile of v0, /device:TPU:0, one launch (start us, length us, event | category | flops | bytes accessed | tf_op | source)
XLA Modules:
  0.0 365.0 jit_solution(11324183408643841926)
XLA Ops:
  0.6 0.9 slice_bitcast_fusion.11
  1.6 1.7 select_reduce_fusion
  4.2 4.9 %collective-permute-start = (f32[6,1,16,128]{3,2,1,0:T(8,128)S(1)}, f32[6,1,16,128]{3,2,1,0:T(8,128)S(1)}, u32[]{:S(2)}, u32[]{:S(2)}) collective-permute-start(f32[6,1,16,128]{3,2,1,0:T(8,128)S(1)} %get-tuple-element.39), channel_id=1, source_target_pairs={{0,16},{1,17},{2,18},{3,19},{4,20},{5,21},{6,22},{7,23},{8,24},{9,... | collective-permute-start | bytes 147464 | tf_op jit(solution)/shard_map/ppermute | solution.py:44
  9.1 1.3 collective-permute-start.1
  11.4 3.7 %collective-permute-done.1 = f32[6,1,16,128]{3,2,1,0:T(8,128)S(1)} collective-permute-done((f32[6,1,16,128]{3,2,1,0:T(8,128)S(1)}, f32[6,1,16,128]{3,2,1,0:T(8,128)S(1)}, u32[]{:S(2)}, u32[]{:S(2)}) %collective-permute-start.1) | collective-permute-done | bytes 49184 | tf_op jit(solution)/shard_map/ppermute | solution.py:46
  15.1 3.5 collective-permute-start.2
  18.6 1.3 collective-permute-start.3
  20.2 4.2 %collective-permute-done.3 = f32[6,10,1,128]{3,2,1,0:T(1,128)S(1)} collective-permute-done((f32[6,10,1,128]{3,2,1,0:T(1,128)S(1)}, f32[6,10,1,128]{3,2,1,0:T(1,128)S(1)}, u32[]{:S(2)}, u32[]{:S(2)}) %collective-permute-start.3) | collective-permute-done | bytes 30752 | tf_op jit(solution)/shard_map/ppermute | solution.py:46
  25.2 1.3 collective-permute-start.4
  27.0 1.3 collective-permute-start.5
  28.8 3.0 collective-permute-done.5
  43.4 40.4 %all-reduce.3 = (f32[64,64]{1,0:T(8,128)S(1)}, f32[64]{0:T(128)S(1)}) all-reduce(f32[64,64]{1,0:T(8,128)S(1)} %convolution_subtract_fusion, f32[64]{0:T(128)S(1)} %convolution_bitcast_fusion.26), channel_id=1, replica_groups=mesh['gx'=2,'gy'=4,'gz'=4] {'gx','gy','gz'}, use_global_device_ids=true, to_apply=%region_7.8 | all-reduce | flops 4160 | bytes 33280 | tf_op jit(solution)/shard_map/psum | solution.py:154
  84.0 5.8 %cholesky.19 = f32[64,64]{1,0:T(8,128)S(1)} custom-call(f32[64,64]{1,0:T(8,128)S(1)} %fusion.262), custom_call_target="Cholesky" | custom-call | tf_op jit(solution)/shard_map/jit(cholesky)/cholesky | solution.py:156
  91.2 4.9 %custom-call.11 = f32[1,64,64]{1,2,0:T(8,128)S(1)} custom-call(f32[1,64,64]{2,1,0:T(8,128)S(1)} %fusion.251), custom_call_target="InvertDiagBlocksLowerTriangular" | custom-call | tf_op jit(solution)/shard_map/jit(_cho_solve)/triangular_solve | solution.py:172
  96.8 1.3 collective-permute-start.6
  98.1 4.5 %collective-permute-start.7 = (f32[1,16,128]{2,1,0:T(8,128)S(1)}, f32[1,16,128]{2,1,0:T(8,128)S(1)}, u32[]{:S(2)}, u32[]{:S(2)}) collective-permute-start(f32[1,16,128]{2,1,0:T(8,128)S(1)} %slice.1082), channel_id=1, source_target_pairs={{0,16},{1,17},{2,18},{3,19},{4,20},{5,21},{6,22},{7,23},{8,24},{9,... | collective-permute-start | bytes 24584 | tf_op jit(solution)/shard_map/ppermute | solution.py:44
  102.6 1.3 collective-permute-done.7
  104.0 1.3 collective-permute-start.8
  105.3 4.5 %collective-permute-start.9 = (f32[10,1,128]{2,1,0:T(1,128)S(1)}, f32[10,1,128]{2,1,0:T(1,128)S(1)}, u32[]{:S(2)}, u32[]{:S(2)}) collective-permute-start(f32[10,1,128]{2,1,0:T(1,128)S(1)} %get-tuple-element.105), channel_id=1, source_target_pairs={{0,4},{4,8},{8,12},{1,5},{5,9},{9,13},{2,6},{6,10},{10,14},{3,7},{... | collective-permute-start | bytes 15368 | tf_op jit(solution)/shard_map/ppermute | solution.py:44
  109.9 1.3 collective-permute-done.9
  111.3 1.3 collective-permute-start.10
  112.6 3.0 collective-permute-start.11
  115.7 0.9 collective-permute-done.11
  117.0 1.3 collective-permute-start.12
  118.3 4.5 %collective-permute-start.13 = (f32[1,16,128]{2,1,0:T(8,128)S(1)}, f32[1,16,128]{2,1,0:T(8,128)S(1)}, u32[]{:S(2)}, u32[]{:S(2)}) collective-permute-start(f32[1,16,128]{2,1,0:T(8,128)S(1)} %get-tuple-element.111), channel_id=1, source_target_pairs={{0,16},{1,17},{2,18},{3,19},{4,20},{5,21},{6,22},{7,23},{8,24},{9,... | collective-permute-start | bytes 24584 | tf_op jit(solution)/shard_map/ppermute | solution.py:44
  122.9 1.3 collective-permute-done.13
  124.2 1.3 collective-permute-start.14
  125.5 4.8 %collective-permute-start.15 = (f32[10,1,128]{2,1,0:T(1,128)S(1)}, f32[10,1,128]{2,1,0:T(1,128)S(1)}, u32[]{:S(2)}, u32[]{:S(2)}) collective-permute-start(f32[10,1,128]{2,1,0:T(1,128)S(1)} %get-tuple-element.101), channel_id=1, source_target_pairs={{0,4},{4,8},{8,12},{1,5},{5,9},{9,13},{2,6},{6,10},{10,14},{3,7},{... | collective-permute-start | bytes 15368 | tf_op jit(solution)/shard_map/ppermute | solution.py:44
  130.3 1.3 collective-permute-done.15
  131.8 1.3 collective-permute-start.16
  133.1 3.3 collective-permute-start.17
  136.5 0.9 collective-permute-done.17
  138.8 48.9 %all-reduce.2 = (f32[64]{0:T(128)S(1)}, f32[]{:T(128)}, f32[]{:T(128)}) all-reduce(f32[64]{0:T(128)S(1)} %convolution_bitcast_fusion.24, f32[]{:T(128)} %get-tuple-element.10, f32[]{:T(128)} %get-tuple-element.8), channel_id=1, replica_groups=mesh['gx'=2,'gy'=4,'gz'=4] {'gx','gy','gz'}, use_global_device_ids=true, to_apply=%region_19.21 | all-reduce | flops 66 | bytes 528 | tf_op jit(solution)/shard_map/psum | solution.py:185
  189.0 1.3 collective-permute-start.18
  190.3 4.5 %collective-permute-start.19 = (f32[1,16,128]{2,1,0:T(8,128)S(1)}, f32[1,16,128]{2,1,0:T(8,128)S(1)}, u32[]{:S(2)}, u32[]{:S(2)}) collective-permute-start(f32[1,16,128]{2,1,0:T(8,128)S(1)} %slice.1129), channel_id=1, source_target_pairs={{0,16},{1,17},{2,18},{3,19},{4,20},{5,21},{6,22},{7,23},{8,24},{9,... | collective-permute-start | bytes 24584 | tf_op jit(solution)/shard_map/ppermute | solution.py:44
  194.9 1.3 collective-permute-done.19
  196.2 1.3 collective-permute-start.20
  197.5 4.5 %collective-permute-start.21 = (f32[10,1,128]{2,1,0:T(1,128)S(1)}, f32[10,1,128]{2,1,0:T(1,128)S(1)}, u32[]{:S(2)}, u32[]{:S(2)}) collective-permute-start(f32[10,1,128]{2,1,0:T(1,128)S(1)} %get-tuple-element.97), channel_id=1, source_target_pairs={{0,4},{4,8},{8,12},{1,5},{5,9},{9,13},{2,6},{6,10},{10,14},{3,7},{... | collective-permute-start | bytes 15368 | tf_op jit(solution)/shard_map/ppermute | solution.py:44
  204.2 1.3 collective-permute-start.22
  205.5 3.0 collective-permute-start.23
  208.6 0.9 collective-permute-done.23
  209.9 1.3 collective-permute-start.24
  211.2 4.5 %collective-permute-start.25 = (f32[1,16,128]{2,1,0:T(8,128)S(1)}, f32[1,16,128]{2,1,0:T(8,128)S(1)}, u32[]{:S(2)}, u32[]{:S(2)}) collective-permute-start(f32[1,16,128]{2,1,0:T(8,128)S(1)} %get-tuple-element.109), channel_id=1, source_target_pairs={{0,16},{1,17},{2,18},{3,19},{4,20},{5,21},{6,22},{7,23},{8,24},{9,... | collective-permute-start | bytes 24584 | tf_op jit(solution)/shard_map/ppermute | solution.py:44
  215.7 1.3 collective-permute-done.25
  217.1 1.3 collective-permute-start.26
  218.4 4.5 %collective-permute-start.27 = (f32[10,1,128]{2,1,0:T(1,128)S(1)}, f32[10,1,128]{2,1,0:T(1,128)S(1)}, u32[]{:S(2)}, u32[]{:S(2)}) collective-permute-start(f32[10,1,128]{2,1,0:T(1,128)S(1)} %get-tuple-element.93), channel_id=1, source_target_pairs={{0,4},{4,8},{8,12},{1,5},{5,9},{9,13},{2,6},{6,10},{10,14},{3,7},{... | collective-permute-start | bytes 15368 | tf_op jit(solution)/shard_map/ppermute | solution.py:44
  223.0 1.3 collective-permute-done.27
  224.4 1.3 collective-permute-start.28
  225.7 3.2 collective-permute-start.29
  229.0 0.9 collective-permute-done.29
  231.3 48.6 %all-reduce.1 = (f32[]{:T(128)}, f32[]{:T(128)}, f32[64]{0:T(128)S(1)}) all-reduce(f32[]{:T(128)} %get-tuple-element.7, f32[]{:T(128)} %get-tuple-element.6, f32[64]{0:T(128)S(1)} %convolution_bitcast_fusion.22), channel_id=1, replica_groups=mesh['gx'=2,'gy'=4,'gz'=4] {'gx','gy','gz'}, use_global_device_ids=true, to_apply=%region_22.24 | all-reduce | flops 66 | bytes 528 | tf_op jit(solution)/shard_map/psum | solution.py:185
  281.3 1.3 collective-permute-start.36
  282.6 4.5 %collective-permute-start.37 = (f32[1,16,128]{2,1,0:T(8,128)S(1)}, f32[1,16,128]{2,1,0:T(8,128)S(1)}, u32[]{:S(2)}, u32[]{:S(2)}) collective-permute-start(f32[1,16,128]{2,1,0:T(8,128)S(1)} %slice.1200), channel_id=1, source_target_pairs={{0,16},{1,17},{2,18},{3,19},{4,20},{5,21},{6,22},{7,23},{8,24},{9,... | collective-permute-start | bytes 24584 | tf_op jit(solution)/shard_map/ppermute | solution.py:44
  291.7 1.3 collective-permute-start.30
  293.0 4.5 %collective-permute-start.31 = (f32[1,16,128]{2,1,0:T(8,128)S(1)}, f32[1,16,128]{2,1,0:T(8,128)S(1)}, u32[]{:S(2)}, u32[]{:S(2)}) collective-permute-start(f32[1,16,128]{2,1,0:T(8,128)S(1)} %get-tuple-element.107), channel_id=1, source_target_pairs={{0,16},{1,17},{2,18},{3,19},{4,20},{5,21},{6,22},{7,23},{8,24},{9,... | collective-permute-start | bytes 24584 | tf_op jit(solution)/shard_map/ppermute | solution.py:44
  297.6 1.3 collective-permute-start.38
  298.9 4.5 %collective-permute-start.39 = (f32[10,1,128]{2,1,0:T(1,128)S(1)}, f32[10,1,128]{2,1,0:T(1,128)S(1)}, u32[]{:S(2)}, u32[]{:S(2)}) collective-permute-start(f32[10,1,128]{2,1,0:T(1,128)S(1)} %get-tuple-element.85), channel_id=1, source_target_pairs={{0,4},{4,8},{8,12},{1,5},{5,9},{9,13},{2,6},{6,10},{10,14},{3,7},{... | collective-permute-start | bytes 15368 | tf_op jit(solution)/shard_map/ppermute | solution.py:44
  303.5 1.3 collective-permute-start.32
  304.8 4.5 %collective-permute-start.33 = (f32[10,1,128]{2,1,0:T(1,128)S(1)}, f32[10,1,128]{2,1,0:T(1,128)S(1)}, u32[]{:S(2)}, u32[]{:S(2)}) collective-permute-start(f32[10,1,128]{2,1,0:T(1,128)S(1)} %get-tuple-element.89), channel_id=1, source_target_pairs={{0,4},{4,8},{8,12},{1,5},{5,9},{9,13},{2,6},{6,10},{10,14},{3,7},{... | collective-permute-start | bytes 15368 | tf_op jit(solution)/shard_map/ppermute | solution.py:44
  309.5 1.3 collective-permute-start.40
  310.8 3.0 collective-permute-start.41
  314.0 1.3 collective-permute-start.34
  315.3 4.7 %collective-permute-start.35 = (f32[10,18,1]{2,1,0:T(8,128)S(1)}, f32[10,18,1]{2,1,0:T(8,128)S(1)}, u32[]{:S(2)}, u32[]{:S(2)}) collective-permute-start(f32[10,18,1]{2,1,0:T(8,128)S(1)} %get-tuple-element.61), channel_id=1, source_target_pairs={{0,1},{1,2},{2,3},{4,5},{5,6},{6,7},{8,9},{9,10},{10,11},{12,13},{... | collective-permute-start | bytes 2168 | tf_op jit(solution)/shard_map/ppermute | solution.py:44
  321.7 40.9 %psum.71 = f32[64]{0:T(128)S(1)} all-reduce(f32[64]{0:T(128)S(1)} %convolution_bitcast_fusion.21), channel_id=1, replica_groups=mesh['gx'=2,'gy'=4,'gz'=4] {'gx','gy','gz'}, use_global_device_ids=true, to_apply=%region_31.33 | all-reduce | flops 64 | bytes 512 | tf_op jit(solution)/shard_map/psum | solution.py:171
  (216 shorter events, 28.7 us)
Async XLA Ops:
  0.6 10.1 %copy-start = (f32[8,16,128]{2,1,0:T(8,128)S(1)}, f32[8,16,128]{2,1,0:T(8,128)}, u32[]{:S(2)}) copy-start(f32[8,16,128]{2,1,0:T(8,128)} %param.7) | copy-start | bytes 196612
  0.6 10.3 %copy-start.1 = (s32[2,4,8]{2,1,0:T(4,128)S(1)}, s32[2,4,8]{2,1,0:T(4,128)}, u32[]{:S(2)}) copy-start(s32[2,4,8]{2,1,0:T(4,128)} %param.11) | copy-start | bytes 772
  4.2 7.1 %collective-permute-start = (f32[6,1,16,128]{3,2,1,0:T(8,128)S(1)}, f32[6,1,16,128]{3,2,1,0:T(8,128)S(1)}, u32[]{:S(2)}, u32[]{:S(2)}) collective-permute-start(f32[6,1,16,128]{3,2,1,0:T(8,128)S(1)} %get-tuple-element.39), channel_id=1, source_target_pairs={{0,16},{1,17},{2,18},{3,19},{4,20},{5,21},{6,22},{7,23},{8,24},{9,... | collective-permute-start | bytes 147464 | tf_op jit(solution)/shard_map/ppermute | solution.py:44
  9.1 6.0 %collective-permute-start.1 = (f32[6,1,16,128]{3,2,1,0:T(8,128)S(1)}, f32[6,1,16,128]{3,2,1,0:T(8,128)S(1)}, u32[]{:S(2)}, u32[]{:S(2)}) collective-permute-start(f32[6,1,16,128]{3,2,1,0:T(8,128)S(1)} %get-tuple-element.40), channel_id=1, source_target_pairs={{16,0},{17,1},{18,2},{19,3},{20,4},{21,5},{22,6},{23,7},{24,8},{25... | collective-permute-start | bytes 147464 | tf_op jit(solution)/shard_map/ppermute | solution.py:46
  15.1 5.0 %collective-permute-start.2 = (f32[6,10,1,128]{3,2,1,0:T(1,128)S(1)}, f32[6,10,1,128]{3,2,1,0:T(1,128)S(1)}, u32[]{:S(2)}, u32[]{:S(2)}) collective-permute-start(f32[6,10,1,128]{3,2,1,0:T(1,128)S(1)} %get-tuple-element.37), channel_id=1, source_target_pairs={{0,4},{4,8},{8,12},{1,5},{5,9},{9,13},{2,6},{6,10},{10,14},{3,7},{... | collective-permute-start | bytes 92168 | tf_op jit(solution)/shard_map/ppermute | solution.py:44
  18.6 5.8 %collective-permute-start.3 = (f32[6,10,1,128]{3,2,1,0:T(1,128)S(1)}, f32[6,10,1,128]{3,2,1,0:T(1,128)S(1)}, u32[]{:S(2)}, u32[]{:S(2)}) collective-permute-start(f32[6,10,1,128]{3,2,1,0:T(1,128)S(1)} %get-tuple-element.38), channel_id=1, source_target_pairs={{4,0},{8,4},{12,8},{5,1},{9,5},{13,9},{6,2},{10,6},{14,10},{7,3},{... | collective-permute-start | bytes 92168 | tf_op jit(solution)/shard_map/ppermute | solution.py:46
  25.2 3.1 collective-permute-start.4
  27.0 4.8 %collective-permute-start.5 = (f32[6,10,18,1]{2,3,1,0:T(1,128)S(1)}, f32[6,10,18,1]{2,3,1,0:T(1,128)S(1)}, u32[]{:S(2)}, u32[]{:S(2)}) collective-permute-start(f32[6,10,18,1]{2,3,1,0:T(1,128)S(1)} %copy.84), channel_id=1, source_target_pairs={{1,0},{2,1},{3,2},{5,4},{6,5},{7,6},{9,8},{10,9},{11,10},{13,12},{... | collective-permute-start | bytes 12968 | tf_op jit(solution)/shard_map/ppermute | solution.py:46
  96.8 5.9 %collective-permute-start.6 = (f32[1,16,128]{2,1,0:T(8,128)S(1)}, f32[1,16,128]{2,1,0:T(8,128)S(1)}, u32[]{:S(2)}, u32[]{:S(2)}) collective-permute-start(f32[1,16,128]{2,1,0:T(8,128)S(1)} %slice.1082), channel_id=1, source_target_pairs={{16,0},{17,1},{18,2},{19,3},{20,4},{21,5},{22,6},{23,7},{24,8},{25... | collective-permute-start | bytes 24584 | tf_op jit(solution)/shard_map/ppermute | solution.py:46
  98.1 5.9 %collective-permute-start.7 = (f32[1,16,128]{2,1,0:T(8,128)S(1)}, f32[1,16,128]{2,1,0:T(8,128)S(1)}, u32[]{:S(2)}, u32[]{:S(2)}) collective-permute-start(f32[1,16,128]{2,1,0:T(8,128)S(1)} %slice.1082), channel_id=1, source_target_pairs={{0,16},{1,17},{2,18},{3,19},{4,20},{5,21},{6,22},{7,23},{8,24},{9,... | collective-permute-start | bytes 24584 | tf_op jit(solution)/shard_map/ppermute | solution.py:44
  104.0 5.9 %collective-permute-start.8 = (f32[10,1,128]{2,1,0:T(1,128)S(1)}, f32[10,1,128]{2,1,0:T(1,128)S(1)}, u32[]{:S(2)}, u32[]{:S(2)}) collective-permute-start(f32[10,1,128]{2,1,0:T(1,128)S(1)} %get-tuple-element.106), channel_id=1, source_target_pairs={{4,0},{8,4},{12,8},{5,1},{9,5},{13,9},{6,2},{10,6},{14,10},{7,3},{... | collective-permute-start | bytes 15368 | tf_op jit(solution)/shard_map/ppermute | solution.py:46
  105.3 5.9 %collective-permute-start.9 = (f32[10,1,128]{2,1,0:T(1,128)S(1)}, f32[10,1,128]{2,1,0:T(1,128)S(1)}, u32[]{:S(2)}, u32[]{:S(2)}) collective-permute-start(f32[10,1,128]{2,1,0:T(1,128)S(1)} %get-tuple-element.105), channel_id=1, source_target_pairs={{0,4},{4,8},{8,12},{1,5},{5,9},{9,13},{2,6},{6,10},{10,14},{3,7},{... | collective-permute-start | bytes 15368 | tf_op jit(solution)/shard_map/ppermute | solution.py:44
  111.3 4.4 %collective-permute-start.10 = (f32[10,18,1]{2,1,0:T(8,128)S(1)}, f32[10,18,1]{2,1,0:T(8,128)S(1)}, u32[]{:S(2)}, u32[]{:S(2)}) collective-permute-start(f32[10,18,1]{2,1,0:T(8,128)S(1)} %get-tuple-element.70), channel_id=1, source_target_pairs={{1,0},{2,1},{3,2},{5,4},{6,5},{7,6},{9,8},{10,9},{11,10},{13,12},{... | collective-permute-start | bytes 2168 | tf_op jit(solution)/shard_map/ppermute | solution.py:46
  112.6 4.0 %collective-permute-start.11 = (f32[10,18,1]{2,1,0:T(8,128)S(1)}, f32[10,18,1]{2,1,0:T(8,128)S(1)}, u32[]{:S(2)}, u32[]{:S(2)}) collective-permute-start(f32[10,18,1]{2,1,0:T(8,128)S(1)} %get-tuple-element.69), channel_id=1, source_target_pairs={{0,1},{1,2},{2,3},{4,5},{5,6},{6,7},{8,9},{9,10},{10,11},{12,13},{... | collective-permute-start | bytes 2168 | tf_op jit(solution)/shard_map/ppermute | solution.py:44
  117.0 5.9 %collective-permute-start.12 = (f32[1,16,128]{2,1,0:T(8,128)S(1)}, f32[1,16,128]{2,1,0:T(8,128)S(1)}, u32[]{:S(2)}, u32[]{:S(2)}) collective-permute-start(f32[1,16,128]{2,1,0:T(8,128)S(1)} %get-tuple-element.112), channel_id=1, source_target_pairs={{16,0},{17,1},{18,2},{19,3},{20,4},{21,5},{22,6},{23,7},{24,8},{25... | collective-permute-start | bytes 24584 | tf_op jit(solution)/shard_map/ppermute | solution.py:46
  118.3 5.9 %collective-permute-start.13 = (f32[1,16,128]{2,1,0:T(8,128)S(1)}, f32[1,16,128]{2,1,0:T(8,128)S(1)}, u32[]{:S(2)}, u32[]{:S(2)}) collective-permute-start(f32[1,16,128]{2,1,0:T(8,128)S(1)} %get-tuple-element.111), channel_id=1, source_target_pairs={{0,16},{1,17},{2,18},{3,19},{4,20},{5,21},{6,22},{7,23},{8,24},{9,... | collective-permute-start | bytes 24584 | tf_op jit(solution)/shard_map/ppermute | solution.py:44
  124.2 6.1 %collective-permute-start.14 = (f32[10,1,128]{2,1,0:T(1,128)S(1)}, f32[10,1,128]{2,1,0:T(1,128)S(1)}, u32[]{:S(2)}, u32[]{:S(2)}) collective-permute-start(f32[10,1,128]{2,1,0:T(1,128)S(1)} %get-tuple-element.102), channel_id=1, source_target_pairs={{4,0},{8,4},{12,8},{5,1},{9,5},{13,9},{6,2},{10,6},{14,10},{7,3},{... | collective-permute-start | bytes 15368 | tf_op jit(solution)/shard_map/ppermute | solution.py:46
  125.5 6.1 %collective-permute-start.15 = (f32[10,1,128]{2,1,0:T(1,128)S(1)}, f32[10,1,128]{2,1,0:T(1,128)S(1)}, u32[]{:S(2)}, u32[]{:S(2)}) collective-permute-start(f32[10,1,128]{2,1,0:T(1,128)S(1)} %get-tuple-element.101), channel_id=1, source_target_pairs={{0,4},{4,8},{8,12},{1,5},{5,9},{9,13},{2,6},{6,10},{10,14},{3,7},{... | collective-permute-start | bytes 15368 | tf_op jit(solution)/shard_map/ppermute | solution.py:44
  131.8 4.7 %collective-permute-start.16 = (f32[10,18,1]{2,1,0:T(8,128)S(1)}, f32[10,18,1]{2,1,0:T(8,128)S(1)}, u32[]{:S(2)}, u32[]{:S(2)}) collective-permute-start(f32[10,18,1]{2,1,0:T(8,128)S(1)} %get-tuple-element.68), channel_id=1, source_target_pairs={{1,0},{2,1},{3,2},{5,4},{6,5},{7,6},{9,8},{10,9},{11,10},{13,12},{... | collective-permute-start | bytes 2168 | tf_op jit(solution)/shard_map/ppermute | solution.py:46
  133.1 4.3 %collective-permute-start.17 = (f32[10,18,1]{2,1,0:T(8,128)S(1)}, f32[10,18,1]{2,1,0:T(8,128)S(1)}, u32[]{:S(2)}, u32[]{:S(2)}) collective-permute-start(f32[10,18,1]{2,1,0:T(8,128)S(1)} %get-tuple-element.67), channel_id=1, source_target_pairs={{0,1},{1,2},{2,3},{4,5},{5,6},{6,7},{8,9},{9,10},{10,11},{12,13},{... | collective-permute-start | bytes 2168 | tf_op jit(solution)/shard_map/ppermute | solution.py:44
  189.0 5.8 %collective-permute-start.18 = (f32[1,16,128]{2,1,0:T(8,128)S(1)}, f32[1,16,128]{2,1,0:T(8,128)S(1)}, u32[]{:S(2)}, u32[]{:S(2)}) collective-permute-start(f32[1,16,128]{2,1,0:T(8,128)S(1)} %slice.1129), channel_id=1, source_target_pairs={{16,0},{17,1},{18,2},{19,3},{20,4},{21,5},{22,6},{23,7},{24,8},{25... | collective-permute-start | bytes 24584 | tf_op jit(solution)/shard_map/ppermute | solution.py:46
  190.3 5.9 %collective-permute-start.19 = (f32[1,16,128]{2,1,0:T(8,128)S(1)}, f32[1,16,128]{2,1,0:T(8,128)S(1)}, u32[]{:S(2)}, u32[]{:S(2)}) collective-permute-start(f32[1,16,128]{2,1,0:T(8,128)S(1)} %slice.1129), channel_id=1, source_target_pairs={{0,16},{1,17},{2,18},{3,19},{4,20},{5,21},{6,22},{7,23},{8,24},{9,... | collective-permute-start | bytes 24584 | tf_op jit(solution)/shard_map/ppermute | solution.py:44
  196.2 7.8 %collective-permute-start.20 = (f32[10,1,128]{2,1,0:T(1,128)S(1)}, f32[10,1,128]{2,1,0:T(1,128)S(1)}, u32[]{:S(2)}, u32[]{:S(2)}) collective-permute-start(f32[10,1,128]{2,1,0:T(1,128)S(1)} %get-tuple-element.98), channel_id=1, source_target_pairs={{4,0},{8,4},{12,8},{5,1},{9,5},{13,9},{6,2},{10,6},{14,10},{7,3},{... | collective-permute-start | bytes 15368 | tf_op jit(solution)/shard_map/ppermute | solution.py:46
  197.5 6.5 %collective-permute-start.21 = (f32[10,1,128]{2,1,0:T(1,128)S(1)}, f32[10,1,128]{2,1,0:T(1,128)S(1)}, u32[]{:S(2)}, u32[]{:S(2)}) collective-permute-start(f32[10,1,128]{2,1,0:T(1,128)S(1)} %get-tuple-element.97), channel_id=1, source_target_pairs={{0,4},{4,8},{8,12},{1,5},{5,9},{9,13},{2,6},{6,10},{10,14},{3,7},{... | collective-permute-start | bytes 15368 | tf_op jit(solution)/shard_map/ppermute | solution.py:44
  204.2 4.4 %collective-permute-start.22 = (f32[10,18,1]{2,1,0:T(8,128)S(1)}, f32[10,18,1]{2,1,0:T(8,128)S(1)}, u32[]{:S(2)}, u32[]{:S(2)}) collective-permute-start(f32[10,18,1]{2,1,0:T(8,128)S(1)} %get-tuple-element.66), channel_id=1, source_target_pairs={{1,0},{2,1},{3,2},{5,4},{6,5},{7,6},{9,8},{10,9},{11,10},{13,12},{... | collective-permute-start | bytes 2168 | tf_op jit(solution)/shard_map/ppermute | solution.py:46
  205.5 4.0 %collective-permute-start.23 = (f32[10,18,1]{2,1,0:T(8,128)S(1)}, f32[10,18,1]{2,1,0:T(8,128)S(1)}, u32[]{:S(2)}, u32[]{:S(2)}) collective-permute-start(f32[10,18,1]{2,1,0:T(8,128)S(1)} %get-tuple-element.65), channel_id=1, source_target_pairs={{0,1},{1,2},{2,3},{4,5},{5,6},{6,7},{8,9},{9,10},{10,11},{12,13},{... | collective-permute-start | bytes 2168 | tf_op jit(solution)/shard_map/ppermute | solution.py:44
  209.9 5.9 %collective-permute-start.24 = (f32[1,16,128]{2,1,0:T(8,128)S(1)}, f32[1,16,128]{2,1,0:T(8,128)S(1)}, u32[]{:S(2)}, u32[]{:S(2)}) collective-permute-start(f32[1,16,128]{2,1,0:T(8,128)S(1)} %get-tuple-element.110), channel_id=1, source_target_pairs={{16,0},{17,1},{18,2},{19,3},{20,4},{21,5},{22,6},{23,7},{24,8},{25... | collective-permute-start | bytes 24584 | tf_op jit(solution)/shard_map/ppermute | solution.py:46
  211.2 5.9 %collective-permute-start.25 = (f32[1,16,128]{2,1,0:T(8,128)S(1)}, f32[1,16,128]{2,1,0:T(8,128)S(1)}, u32[]{:S(2)}, u32[]{:S(2)}) collective-permute-start(f32[1,16,128]{2,1,0:T(8,128)S(1)} %get-tuple-element.109), channel_id=1, source_target_pairs={{0,16},{1,17},{2,18},{3,19},{4,20},{5,21},{6,22},{7,23},{8,24},{9,... | collective-permute-start | bytes 24584 | tf_op jit(solution)/shard_map/ppermute | solution.py:44
  217.1 5.9 %collective-permute-start.26 = (f32[10,1,128]{2,1,0:T(1,128)S(1)}, f32[10,1,128]{2,1,0:T(1,128)S(1)}, u32[]{:S(2)}, u32[]{:S(2)}) collective-permute-start(f32[10,1,128]{2,1,0:T(1,128)S(1)} %get-tuple-element.94), channel_id=1, source_target_pairs={{4,0},{8,4},{12,8},{5,1},{9,5},{13,9},{6,2},{10,6},{14,10},{7,3},{... | collective-permute-start | bytes 15368 | tf_op jit(solution)/shard_map/ppermute | solution.py:46
  218.4 5.9 %collective-permute-start.27 = (f32[10,1,128]{2,1,0:T(1,128)S(1)}, f32[10,1,128]{2,1,0:T(1,128)S(1)}, u32[]{:S(2)}, u32[]{:S(2)}) collective-permute-start(f32[10,1,128]{2,1,0:T(1,128)S(1)} %get-tuple-element.93), channel_id=1, source_target_pairs={{0,4},{4,8},{8,12},{1,5},{5,9},{9,13},{2,6},{6,10},{10,14},{3,7},{... | collective-permute-start | bytes 15368 | tf_op jit(solution)/shard_map/ppermute | solution.py:44
  224.4 4.6 %collective-permute-start.28 = (f32[10,18,1]{2,1,0:T(8,128)S(1)}, f32[10,18,1]{2,1,0:T(8,128)S(1)}, u32[]{:S(2)}, u32[]{:S(2)}) collective-permute-start(f32[10,18,1]{2,1,0:T(8,128)S(1)} %get-tuple-element.64), channel_id=1, source_target_pairs={{1,0},{2,1},{3,2},{5,4},{6,5},{7,6},{9,8},{10,9},{11,10},{13,12},{... | collective-permute-start | bytes 2168 | tf_op jit(solution)/shard_map/ppermute | solution.py:46
  225.7 4.2 %collective-permute-start.29 = (f32[10,18,1]{2,1,0:T(8,128)S(1)}, f32[10,18,1]{2,1,0:T(8,128)S(1)}, u32[]{:S(2)}, u32[]{:S(2)}) collective-permute-start(f32[10,18,1]{2,1,0:T(8,128)S(1)} %get-tuple-element.63), channel_id=1, source_target_pairs={{0,1},{1,2},{2,3},{4,5},{5,6},{6,7},{8,9},{9,10},{10,11},{12,13},{... | collective-permute-start | bytes 2168 | tf_op jit(solution)/shard_map/ppermute | solution.py:44
  281.3 16.3 %collective-permute-start.36 = (f32[1,16,128]{2,1,0:T(8,128)S(1)}, f32[1,16,128]{2,1,0:T(8,128)S(1)}, u32[]{:S(2)}, u32[]{:S(2)}) collective-permute-start(f32[1,16,128]{2,1,0:T(8,128)S(1)} %slice.1200), channel_id=1, source_target_pairs={{16,0},{17,1},{18,2},{19,3},{20,4},{21,5},{22,6},{23,7},{24,8},{25... | collective-permute-start | bytes 24584 | tf_op jit(solution)/shard_map/ppermute | solution.py:46
  282.6 15.0 %collective-permute-start.37 = (f32[1,16,128]{2,1,0:T(8,128)S(1)}, f32[1,16,128]{2,1,0:T(8,128)S(1)}, u32[]{:S(2)}, u32[]{:S(2)}) collective-permute-start(f32[1,16,128]{2,1,0:T(8,128)S(1)} %slice.1200), channel_id=1, source_target_pairs={{0,16},{1,17},{2,18},{3,19},{4,20},{5,21},{6,22},{7,23},{8,24},{9,... | collective-permute-start | bytes 24584 | tf_op jit(solution)/shard_map/ppermute | solution.py:44
  291.7 11.8 %collective-permute-start.30 = (f32[1,16,128]{2,1,0:T(8,128)S(1)}, f32[1,16,128]{2,1,0:T(8,128)S(1)}, u32[]{:S(2)}, u32[]{:S(2)}) collective-permute-start(f32[1,16,128]{2,1,0:T(8,128)S(1)} %get-tuple-element.108), channel_id=1, source_target_pairs={{16,0},{17,1},{18,2},{19,3},{20,4},{21,5},{22,6},{23,7},{24,8},{25... | collective-permute-start | bytes 24584 | tf_op jit(solution)/shard_map/ppermute | solution.py:46
  293.0 10.5 %collective-permute-start.31 = (f32[1,16,128]{2,1,0:T(8,128)S(1)}, f32[1,16,128]{2,1,0:T(8,128)S(1)}, u32[]{:S(2)}, u32[]{:S(2)}) collective-permute-start(f32[1,16,128]{2,1,0:T(8,128)S(1)} %get-tuple-element.107), channel_id=1, source_target_pairs={{0,16},{1,17},{2,18},{3,19},{4,20},{5,21},{6,22},{7,23},{8,24},{9,... | collective-permute-start | bytes 24584 | tf_op jit(solution)/shard_map/ppermute | solution.py:44
  297.6 11.8 %collective-permute-start.38 = (f32[10,1,128]{2,1,0:T(1,128)S(1)}, f32[10,1,128]{2,1,0:T(1,128)S(1)}, u32[]{:S(2)}, u32[]{:S(2)}) collective-permute-start(f32[10,1,128]{2,1,0:T(1,128)S(1)} %get-tuple-element.86), channel_id=1, source_target_pairs={{4,0},{8,4},{12,8},{5,1},{9,5},{13,9},{6,2},{10,6},{14,10},{7,3},{... | collective-permute-start | bytes 15368 | tf_op jit(solution)/shard_map/ppermute | solution.py:46
  298.9 10.5 %collective-permute-start.39 = (f32[10,1,128]{2,1,0:T(1,128)S(1)}, f32[10,1,128]{2,1,0:T(1,128)S(1)}, u32[]{:S(2)}, u32[]{:S(2)}) collective-permute-start(f32[10,1,128]{2,1,0:T(1,128)S(1)} %get-tuple-element.85), channel_id=1, source_target_pairs={{0,4},{4,8},{8,12},{1,5},{5,9},{9,13},{2,6},{6,10},{10,14},{3,7},{... | collective-permute-start | bytes 15368 | tf_op jit(solution)/shard_map/ppermute | solution.py:44
  303.5 10.3 %collective-permute-start.32 = (f32[10,1,128]{2,1,0:T(1,128)S(1)}, f32[10,1,128]{2,1,0:T(1,128)S(1)}, u32[]{:S(2)}, u32[]{:S(2)}) collective-permute-start(f32[10,1,128]{2,1,0:T(1,128)S(1)} %get-tuple-element.90), channel_id=1, source_target_pairs={{4,0},{8,4},{12,8},{5,1},{9,5},{13,9},{6,2},{10,6},{14,10},{7,3},{... | collective-permute-start | bytes 15368 | tf_op jit(solution)/shard_map/ppermute | solution.py:46
  304.8 9.1 %collective-permute-start.33 = (f32[10,1,128]{2,1,0:T(1,128)S(1)}, f32[10,1,128]{2,1,0:T(1,128)S(1)}, u32[]{:S(2)}, u32[]{:S(2)}) collective-permute-start(f32[10,1,128]{2,1,0:T(1,128)S(1)} %get-tuple-element.89), channel_id=1, source_target_pairs={{0,4},{4,8},{8,12},{1,5},{5,9},{9,13},{2,6},{6,10},{10,14},{3,7},{... | collective-permute-start | bytes 15368 | tf_op jit(solution)/shard_map/ppermute | solution.py:44
  309.5 54.4 %collective-permute-start.40 = (f32[10,18,1]{2,1,0:T(8,128)S(1)}, f32[10,18,1]{2,1,0:T(8,128)S(1)}, u32[]{:S(2)}, u32[]{:S(2)}) collective-permute-start(f32[10,18,1]{2,1,0:T(8,128)S(1)} %get-tuple-element.60), channel_id=1, source_target_pairs={{1,0},{2,1},{3,2},{5,4},{6,5},{7,6},{9,8},{10,9},{11,10},{13,12},{... | collective-permute-start | bytes 2168 | tf_op jit(solution)/shard_map/ppermute | solution.py:46
  310.8 53.1 %collective-permute-start.41 = (f32[10,18,1]{2,1,0:T(8,128)S(1)}, f32[10,18,1]{2,1,0:T(8,128)S(1)}, u32[]{:S(2)}, u32[]{:S(2)}) collective-permute-start(f32[10,18,1]{2,1,0:T(8,128)S(1)} %get-tuple-element.59), channel_id=1, source_target_pairs={{0,1},{1,2},{2,3},{4,5},{5,6},{6,7},{8,9},{9,10},{10,11},{12,13},{... | collective-permute-start | bytes 2168 | tf_op jit(solution)/shard_map/ppermute | solution.py:44
  314.0 6.0 %collective-permute-start.34 = (f32[10,18,1]{2,1,0:T(8,128)S(1)}, f32[10,18,1]{2,1,0:T(8,128)S(1)}, u32[]{:S(2)}, u32[]{:S(2)}) collective-permute-start(f32[10,18,1]{2,1,0:T(8,128)S(1)} %get-tuple-element.62), channel_id=1, source_target_pairs={{1,0},{2,1},{3,2},{5,4},{6,5},{7,6},{9,8},{10,9},{11,10},{13,12},{... | collective-permute-start | bytes 2168 | tf_op jit(solution)/shard_map/ppermute | solution.py:46
  315.3 5.6 %collective-permute-start.35 = (f32[10,18,1]{2,1,0:T(8,128)S(1)}, f32[10,18,1]{2,1,0:T(8,128)S(1)}, u32[]{:S(2)}, u32[]{:S(2)}) collective-permute-start(f32[10,18,1]{2,1,0:T(8,128)S(1)} %get-tuple-element.61), channel_id=1, source_target_pairs={{0,1},{1,2},{2,3},{4,5},{5,6},{6,7},{8,9},{9,10},{10,11},{12,13},{... | collective-permute-start | bytes 2168 | tf_op jit(solution)/shard_map/ppermute | solution.py:44
where the time goes:
time: 367 us; the launch traced here: 365 us
  blocking collectives  179 us (49%)
  starting transfers between devices  112 us (31%)
  waiting for transfers between devices  25.1 us (7%)
  other arithmetic  22.3 us (6%)
  matrix products  13.4 us (4%)
  between operations  8.31 us (2%)
  local copies, waits for them, and re-layouts  5.09 us (1%)
    psum x2, blocking collectives, joint_terms(): lax.psum((restrict(product), jnp.sum(field * field), jnp.sum(field * prod...  97.5 us
    ppermute x21, starting transfers between devices, padded_2(): lax.ppermute(tail, axis, [(i, (i + 1) % count) for i in range(ends)])  84.8 us
    psum x1, blocking collectives, coarse_solve(): projected = lax.psum(restrict(field), ('gx', 'gy', 'gz'))  40.9 us
    psum x1, blocking collectives, body(): coarse = lax.psum(jnp.diag(diagonal_terms) - coupling, ('gx', 'gy', 'gz'))  40.4 us
    ppermute x21, starting transfers between devices, padded_2(): lax.ppermute(head, axis, [((i + 1) % count, i) for i in range(ends)])  27.1 us
    ppermute x21, waiting for transfers between devices, padded_2(): lax.ppermute(tail, axis, [(i, (i + 1) % count) for i in range(ends)])  14.1 us
    ppermute x21, waiting for transfers between devices, padded_2(): lax.ppermute(head, axis, [((i + 1) % count, i) for i in range(ends)])  11 us
    dot_general x54, matrix products, body(): jnp.einsum('xyz,xa,yb,zjc->jabc', weight, reach_onehot(CX, step_x), reach...  8.59 us
  transfers between devices with their start and end apart: 42, of which 16 were waited for; matrix products, arithmetic and copies ran while one was open for 1% of the time, Pallas kernels for 0%

commit v1 on v0

--- a/solution.py
+++ b/solution.py
@@ -151,7 +151,9 @@
         class_onehot(neighbours, COARSE),
         precision=highest,
     )
-    coarse = lax.psum(jnp.diag(diagonal_terms) - coupling, ("gx", "gy", "gz"))
+    coarse = jnp.diag(diagonal_terms) - coupling
+    for over in (("gy", "gz"), "gx"):
+        coarse = lax.psum(coarse, over)
     coarse = 0.5 * (coarse + coarse.T)
     factor_lower = jnp.linalg.cholesky(coarse)
 

time: 367 us -> 431 us (1.17)
  blocking collectives: 179 us -> 246 us
    psum x1 -> x2, blocking collectives: 40.9 us -> 82.7 us  [coarse_solve(): projected = lax.psum(restrict(field), ('gx', 'gy', 'gz'))]
    psum x1 -> x2, blocking collectives: 40.4 us -> 67.5 us  [body(): coarse = lax.psum(coarse, over)]
  transfers between devices with their start and end apart: 42 -> 42, of which waited for: 16 -> 15; matrix products, arithmetic and copies ran while one was open for 1% -> 1% of each run, Pallas kernels for 0% -> 0%
where the time goes in v1:
time: 431 us; the launch traced here: 429 us
  blocking collectives  246 us (57%)
  starting transfers between devices  112 us (26%)
  other arithmetic  22.3 us (5%)
  waiting for transfers between devices  21.9 us (5%)
  matrix products  13.4 us (3%)
  between operations  8.3 us (2%)
  local copies, waits for them, and re-layouts  5.09 us (1%)
    psum x2, blocking collectives, joint_terms(): lax.psum((restrict(product), jnp.sum(field * field), jnp.sum(field * prod...  95.8 us
    ppermute x21, starting transfers between devices, padded_2(): lax.ppermute(tail, axis, [(i, (i + 1) % count) for i in range(ends)])  84.7 us
    psum x2, blocking collectives, coarse_solve(): projected = lax.psum(restrict(field), ('gx', 'gy', 'gz'))  82.7 us
    psum x2, blocking collectives, body(): coarse = lax.psum(coarse, over)  67.5 us
    ppermute x21, starting transfers between devices, padded_2(): lax.ppermute(head, axis, [((i + 1) % count, i) for i in range(ends)])  27.1 us
    ppermute x21, waiting for transfers between devices, padded_2(): lax.ppermute(tail, axis, [(i, (i + 1) % count) for i in range(ends)])  13.9 us
  transfers between devices with their start and end apart: 42, of which 15 were waited for; matrix products, arithmetic and copies ran while one was open for 1% of the time, Pallas kernels for 0%

profile of v1, /device:TPU:0, one launch (start us, length us, event | category | flops | bytes accessed | tf_op | source)
XLA Modules:
  0.0 428.9 jit_solution(11072835120044480315)
XLA Ops:
  0.6 0.9 slice_bitcast_fusion.11
  1.6 1.7 select_reduce_fusion
  4.2 4.9 %collective-permute-start = (f32[6,1,16,128]{3,2,1,0:T(8,128)S(1)}, f32[6,1,16,128]{3,2,1,0:T(8,128)S(1)}, u32[]{:S(2)}, u32[]{:S(2)}) collective-permute-start(f32[6,1,16,128]{3,2,1,0:T(8,128)S(1)} %get-tuple-element.37), channel_id=1, source_target_pairs={{0,16},{1,17},{2,18},{3,19},{4,20},{5,21},{6,22},{7,23},{8,24},{9,... | collective-permute-start | bytes 147464 | tf_op jit(solution)/shard_map/ppermute | solution.py:44
  9.1 1.3 collective-permute-start.1
  11.4 3.7 collective-permute-done.1
  15.1 3.5 collective-permute-start.2
  18.6 1.3 collective-permute-start.3
  20.2 4.2 collective-permute-done.3
  25.2 1.3 collective-permute-start.4
  27.0 1.3 collective-permute-start.5
  28.3 42.0 %psum.72 = f32[64]{0:T(128)S(1)} all-reduce(f32[64]{0:T(128)S(1)} %convolution_bitcast_fusion.26), channel_id=1, replica_groups=mesh['gx'=2,'gy'=4,'gz'=4] {'gx','gy','gz'}, use_global_device_ids=true, to_apply=%region_13.14 | all-reduce | flops 64 | bytes 512 | tf_op jit(solution)/shard_map/psum | solution.py:173
  82.4 60.6 %psum.70 = f32[64,64]{1,0:T(8,128)S(1)} all-reduce(f32[64,64]{1,0:T(8,128)S(1)} %convolution_subtract_fusion), channel_id=1, replica_groups=mesh['gx'=2,'gy'=4,'gz'=4] {'gy','gz'}, use_global_device_ids=true, to_apply=%region_7.8 | all-reduce | flops 4096 | bytes 32768 | tf_op jit(solution)/shard_map/psum | solution.py:156
  143.0 6.9 %psum.71 = f32[64,64]{1,0:T(8,128)S(1)} all-reduce(f32[64,64]{1,0:T(8,128)S(1)} %psum.70), channel_id=1, replica_groups=mesh['gx'=2,'gy'=4,'gz'=4] {'gx'}, use_global_device_ids=true, to_apply=%region_8.9 | all-reduce | flops 4096 | bytes 32768 | tf_op jit(solution)/shard_map/psum | solution.py:156
  150.1 5.8 %cholesky.19 = f32[64,64]{1,0:T(8,128)S(1)} custom-call(f32[64,64]{1,0:T(8,128)S(1)} %fusion.262), custom_call_target="Cholesky" | custom-call | tf_op jit(solution)/shard_map/jit(cholesky)/cholesky | solution.py:158
  157.3 4.9 %custom-call.11 = f32[1,64,64]{1,2,0:T(8,128)S(1)} custom-call(f32[1,64,64]{2,1,0:T(8,128)S(1)} %fusion.251), custom_call_target="InvertDiagBlocksLowerTriangular" | custom-call | tf_op jit(solution)/shard_map/jit(_cho_solve)/triangular_solve | solution.py:174
  162.9 1.3 collective-permute-start.6
  164.2 4.5 %collective-permute-start.7 = (f32[1,16,128]{2,1,0:T(8,128)S(1)}, f32[1,16,128]{2,1,0:T(8,128)S(1)}, u32[]{:S(2)}, u32[]{:S(2)}) collective-permute-start(f32[1,16,128]{2,1,0:T(8,128)S(1)} %slice.1082), channel_id=1, source_target_pairs={{0,16},{1,17},{2,18},{3,19},{4,20},{5,21},{6,22},{7,23},{8,24},{9,... | collective-permute-start | bytes 24584 | tf_op jit(solution)/shard_map/ppermute | solution.py:44
  168.7 1.3 collective-permute-done.7
  170.1 1.3 collective-permute-start.8
  171.4 4.5 %collective-permute-start.9 = (f32[10,1,128]{2,1,0:T(1,128)S(1)}, f32[10,1,128]{2,1,0:T(1,128)S(1)}, u32[]{:S(2)}, u32[]{:S(2)}) collective-permute-start(f32[10,1,128]{2,1,0:T(1,128)S(1)} %get-tuple-element.103), channel_id=1, source_target_pairs={{0,4},{4,8},{8,12},{1,5},{5,9},{9,13},{2,6},{6,10},{10,14},{3,7},{... | collective-permute-start | bytes 15368 | tf_op jit(solution)/shard_map/ppermute | solution.py:44
  176.0 1.3 collective-permute-done.9
  177.4 1.3 collective-permute-start.10
  178.7 3.0 collective-permute-start.11
  181.8 0.9 collective-permute-done.11
  183.1 1.3 collective-permute-start.12
  184.4 4.5 %collective-permute-start.13 = (f32[1,16,128]{2,1,0:T(8,128)S(1)}, f32[1,16,128]{2,1,0:T(8,128)S(1)}, u32[]{:S(2)}, u32[]{:S(2)}) collective-permute-start(f32[1,16,128]{2,1,0:T(8,128)S(1)} %get-tuple-element.109), channel_id=1, source_target_pairs={{0,16},{1,17},{2,18},{3,19},{4,20},{5,21},{6,22},{7,23},{8,24},{9,... | collective-permute-start | bytes 24584 | tf_op jit(solution)/shard_map/ppermute | solution.py:44
  189.0 1.3 collective-permute-done.13
  190.3 1.3 collective-permute-start.14
  191.6 4.8 %collective-permute-start.15 = (f32[10,1,128]{2,1,0:T(1,128)S(1)}, f32[10,1,128]{2,1,0:T(1,128)S(1)}, u32[]{:S(2)}, u32[]{:S(2)}) collective-permute-start(f32[10,1,128]{2,1,0:T(1,128)S(1)} %get-tuple-element.99), channel_id=1, source_target_pairs={{0,4},{4,8},{8,12},{1,5},{5,9},{9,13},{2,6},{6,10},{10,14},{3,7},{... | collective-permute-start | bytes 15368 | tf_op jit(solution)/shard_map/ppermute | solution.py:44
  196.4 1.3 collective-permute-done.15
  197.9 1.3 collective-permute-start.16
  199.2 3.2 collective-permute-start.17
  204.6 47.2 %all-reduce.2 = (f32[64]{0:T(128)S(1)}, f32[]{:T(128)}, f32[]{:T(128)}) all-reduce(f32[64]{0:T(128)S(1)} %convolution_bitcast_fusion.24, f32[]{:T(128)} %get-tuple-element.10, f32[]{:T(128)} %get-tuple-element.8), channel_id=1, replica_groups=mesh['gx'=2,'gy'=4,'gz'=4] {'gx','gy','gz'}, use_global_device_ids=true, to_apply=%region_20.22 | all-reduce | flops 66 | bytes 528 | tf_op jit(solution)/shard_map/psum | solution.py:187
  253.1 1.3 collective-permute-start.18
  254.4 4.5 %collective-permute-start.19 = (f32[1,16,128]{2,1,0:T(8,128)S(1)}, f32[1,16,128]{2,1,0:T(8,128)S(1)}, u32[]{:S(2)}, u32[]{:S(2)}) collective-permute-start(f32[1,16,128]{2,1,0:T(8,128)S(1)} %slice.1129), channel_id=1, source_target_pairs={{0,16},{1,17},{2,18},{3,19},{4,20},{5,21},{6,22},{7,23},{8,24},{9,... | collective-permute-start | bytes 24584 | tf_op jit(solution)/shard_map/ppermute | solution.py:44
  259.0 1.3 collective-permute-done.19
  260.3 1.3 collective-permute-start.20
  261.6 4.5 %collective-permute-start.21 = (f32[10,1,128]{2,1,0:T(1,128)S(1)}, f32[10,1,128]{2,1,0:T(1,128)S(1)}, u32[]{:S(2)}, u32[]{:S(2)}) collective-permute-start(f32[10,1,128]{2,1,0:T(1,128)S(1)} %get-tuple-element.95), channel_id=1, source_target_pairs={{0,4},{4,8},{8,12},{1,5},{5,9},{9,13},{2,6},{6,10},{10,14},{3,7},{... | collective-permute-start | bytes 15368 | tf_op jit(solution)/shard_map/ppermute | solution.py:44
  268.3 1.3 collective-permute-start.22
  269.6 3.0 collective-permute-start.23
  272.6 0.9 collective-permute-done.23
  274.0 1.3 collective-permute-start.24
  275.3 4.5 %collective-permute-start.25 = (f32[1,16,128]{2,1,0:T(8,128)S(1)}, f32[1,16,128]{2,1,0:T(8,128)S(1)}, u32[]{:S(2)}, u32[]{:S(2)}) collective-permute-start(f32[1,16,128]{2,1,0:T(8,128)S(1)} %get-tuple-element.107), channel_id=1, source_target_pairs={{0,16},{1,17},{2,18},{3,19},{4,20},{5,21},{6,22},{7,23},{8,24},{9,... | collective-permute-start | bytes 24584 | tf_op jit(solution)/shard_map/ppermute | solution.py:44
  279.8 1.3 collective-permute-done.25
  281.2 1.3 collective-permute-start.26
  282.5 4.5 %collective-permute-start.27 = (f32[10,1,128]{2,1,0:T(1,128)S(1)}, f32[10,1,128]{2,1,0:T(1,128)S(1)}, u32[]{:S(2)}, u32[]{:S(2)}) collective-permute-start(f32[10,1,128]{2,1,0:T(1,128)S(1)} %get-tuple-element.91), channel_id=1, source_target_pairs={{0,4},{4,8},{8,12},{1,5},{5,9},{9,13},{2,6},{6,10},{10,14},{3,7},{... | collective-permute-start | bytes 15368 | tf_op jit(solution)/shard_map/ppermute | solution.py:44
  287.0 1.3 collective-permute-done.27
  288.5 1.3 collective-permute-start.28
  289.8 3.2 collective-permute-start.29
  293.1 0.9 collective-permute-done.29
  295.4 48.6 %all-reduce.1 = (f32[]{:T(128)}, f32[]{:T(128)}, f32[64]{0:T(128)S(1)}) all-reduce(f32[]{:T(128)} %get-tuple-element.7, f32[]{:T(128)} %get-tuple-element.6, f32[64]{0:T(128)S(1)} %convolution_bitcast_fusion.22), channel_id=1, replica_groups=mesh['gx'=2,'gy'=4,'gz'=4] {'gx','gy','gz'}, use_global_device_ids=true, to_apply=%region_23.25 | all-reduce | flops 66 | bytes 528 | tf_op jit(solution)/shard_map/psum | solution.py:187
  345.4 1.3 collective-permute-start.36
  346.7 4.5 %collective-permute-start.37 = (f32[1,16,128]{2,1,0:T(8,128)S(1)}, f32[1,16,128]{2,1,0:T(8,128)S(1)}, u32[]{:S(2)}, u32[]{:S(2)}) collective-permute-start(f32[1,16,128]{2,1,0:T(8,128)S(1)} %slice.1200), channel_id=1, source_target_pairs={{0,16},{1,17},{2,18},{3,19},{4,20},{5,21},{6,22},{7,23},{8,24},{9,... | collective-permute-start | bytes 24584 | tf_op jit(solution)/shard_map/ppermute | solution.py:44
  355.8 1.3 collective-permute-start.30
  357.1 4.5 %collective-permute-start.31 = (f32[1,16,128]{2,1,0:T(8,128)S(1)}, f32[1,16,128]{2,1,0:T(8,128)S(1)}, u32[]{:S(2)}, u32[]{:S(2)}) collective-permute-start(f32[1,16,128]{2,1,0:T(8,128)S(1)} %get-tuple-element.105), channel_id=1, source_target_pairs={{0,16},{1,17},{2,18},{3,19},{4,20},{5,21},{6,22},{7,23},{8,24},{9,... | collective-permute-start | bytes 24584 | tf_op jit(solution)/shard_map/ppermute | solution.py:44
  361.7 1.3 collective-permute-start.38
  363.0 4.5 %collective-permute-start.39 = (f32[10,1,128]{2,1,0:T(1,128)S(1)}, f32[10,1,128]{2,1,0:T(1,128)S(1)}, u32[]{:S(2)}, u32[]{:S(2)}) collective-permute-start(f32[10,1,128]{2,1,0:T(1,128)S(1)} %get-tuple-element.83), channel_id=1, source_target_pairs={{0,4},{4,8},{8,12},{1,5},{5,9},{9,13},{2,6},{6,10},{10,14},{3,7},{... | collective-permute-start | bytes 15368 | tf_op jit(solution)/shard_map/ppermute | solution.py:44
  367.6 1.3 collective-permute-start.32
  368.9 4.5 %collective-permute-start.33 = (f32[10,1,128]{2,1,0:T(1,128)S(1)}, f32[10,1,128]{2,1,0:T(1,128)S(1)}, u32[]{:S(2)}, u32[]{:S(2)}) collective-permute-start(f32[10,1,128]{2,1,0:T(1,128)S(1)} %get-tuple-element.87), channel_id=1, source_target_pairs={{0,4},{4,8},{8,12},{1,5},{5,9},{9,13},{2,6},{6,10},{10,14},{3,7},{... | collective-permute-start | bytes 15368 | tf_op jit(solution)/shard_map/ppermute | solution.py:44
  373.6 1.3 collective-permute-start.40
  374.9 3.0 collective-permute-start.41
  378.1 1.3 collective-permute-start.34
  379.4 4.7 %collective-permute-start.35 = (f32[10,18,1]{2,1,0:T(8,128)S(1)}, f32[10,18,1]{2,1,0:T(8,128)S(1)}, u32[]{:S(2)}, u32[]{:S(2)}) collective-permute-start(f32[10,18,1]{2,1,0:T(8,128)S(1)} %get-tuple-element.59), channel_id=1, source_target_pairs={{0,1},{1,2},{2,3},{4,5},{5,6},{6,7},{8,9},{9,10},{10,11},{12,13},{... | collective-permute-start | bytes 2168 | tf_op jit(solution)/shard_map/ppermute | solution.py:44
  385.8 40.7 %psum.79 = f32[64]{0:T(128)S(1)} all-reduce(f32[64]{0:T(128)S(1)} %convolution_bitcast_fusion.21), channel_id=1, replica_groups=mesh['gx'=2,'gy'=4,'gz'=4] {'gx','gy','gz'}, use_global_device_ids=true, to_apply=%region_32.34 | all-reduce | flops 64 | bytes 512 | tf_op jit(solution)/shard_map/psum | solution.py:173
  (218 shorter events, 29.5 us)
Async XLA Ops:
  0.6 10.1 %copy-start = (f32[8,16,128]{2,1,0:T(8,128)S(1)}, f32[8,16,128]{2,1,0:T(8,128)}, u32[]{:S(2)}) copy-start(f32[8,16,128]{2,1,0:T(8,128)} %param.7) | copy-start | bytes 196612
  0.6 10.3 %copy-start.1 = (s32[2,4,8]{2,1,0:T(4,128)S(1)}, s32[2,4,8]{2,1,0:T(4,128)}, u32[]{:S(2)}) copy-start(s32[2,4,8]{2,1,0:T(4,128)} %param.11) | copy-start | bytes 772
  4.2 7.1 %collective-permute-start = (f32[6,1,16,128]{3,2,1,0:T(8,128)S(1)}, f32[6,1,16,128]{3,2,1,0:T(8,128)S(1)}, u32[]{:S(2)}, u32[]{:S(2)}) collective-permute-start(f32[6,1,16,128]{3,2,1,0:T(8,128)S(1)} %get-tuple-element.37), channel_id=1, source_target_pairs={{0,16},{1,17},{2,18},{3,19},{4,20},{5,21},{6,22},{7,23},{8,24},{9,... | collective-permute-start | bytes 147464 | tf_op jit(solution)/shard_map/ppermute | solution.py:44
  9.1 6.0 %collective-permute-start.1 = (f32[6,1,16,128]{3,2,1,0:T(8,128)S(1)}, f32[6,1,16,128]{3,2,1,0:T(8,128)S(1)}, u32[]{:S(2)}, u32[]{:S(2)}) collective-permute-start(f32[6,1,16,128]{3,2,1,0:T(8,128)S(1)} %get-tuple-element.38), channel_id=1, source_target_pairs={{16,0},{17,1},{18,2},{19,3},{20,4},{21,5},{22,6},{23,7},{24,8},{25... | collective-permute-start | bytes 147464 | tf_op jit(solution)/shard_map/ppermute | solution.py:46
  15.1 5.0 %collective-permute-start.2 = (f32[6,10,1,128]{3,2,1,0:T(1,128)S(1)}, f32[6,10,1,128]{3,2,1,0:T(1,128)S(1)}, u32[]{:S(2)}, u32[]{:S(2)}) collective-permute-start(f32[6,10,1,128]{3,2,1,0:T(1,128)S(1)} %get-tuple-element.35), channel_id=1, source_target_pairs={{0,4},{4,8},{8,12},{1,5},{5,9},{9,13},{2,6},{6,10},{10,14},{3,7},{... | collective-permute-start | bytes 92168 | tf_op jit(solution)/shard_map/ppermute | solution.py:44
  18.6 5.8 %collective-permute-start.3 = (f32[6,10,1,128]{3,2,1,0:T(1,128)S(1)}, f32[6,10,1,128]{3,2,1,0:T(1,128)S(1)}, u32[]{:S(2)}, u32[]{:S(2)}) collective-permute-start(f32[6,10,1,128]{3,2,1,0:T(1,128)S(1)} %get-tuple-element.36), channel_id=1, source_target_pairs={{4,0},{8,4},{12,8},{5,1},{9,5},{13,9},{6,2},{10,6},{14,10},{7,3},{... | collective-permute-start | bytes 92168 | tf_op jit(solution)/shard_map/ppermute | solution.py:46
  25.2 45.1 %collective-permute-start.4 = (f32[6,10,18,1]{2,3,1,0:T(1,128)S(1)}, f32[6,10,18,1]{2,3,1,0:T(1,128)S(1)}, u32[]{:S(2)}, u32[]{:S(2)}) collective-permute-start(f32[6,10,18,1]{2,3,1,0:T(1,128)S(1)} %copy.83), channel_id=1, source_target_pairs={{0,1},{1,2},{2,3},{4,5},{5,6},{6,7},{8,9},{9,10},{10,11},{12,13},{... | collective-permute-start | bytes 12968 | tf_op jit(solution)/shard_map/ppermute | solution.py:44
  27.0 43.8 %collective-permute-start.5 = (f32[6,10,18,1]{2,3,1,0:T(1,128)S(1)}, f32[6,10,18,1]{2,3,1,0:T(1,128)S(1)}, u32[]{:S(2)}, u32[]{:S(2)}) collective-permute-start(f32[6,10,18,1]{2,3,1,0:T(1,128)S(1)} %copy.84), channel_id=1, source_target_pairs={{1,0},{2,1},{3,2},{5,4},{6,5},{7,6},{9,8},{10,9},{11,10},{13,12},{... | collective-permute-start | bytes 12968 | tf_op jit(solution)/shard_map/ppermute | solution.py:46
  162.9 5.9 %collective-permute-start.6 = (f32[1,16,128]{2,1,0:T(8,128)S(1)}, f32[1,16,128]{2,1,0:T(8,128)S(1)}, u32[]{:S(2)}, u32[]{:S(2)}) collective-permute-start(f32[1,16,128]{2,1,0:T(8,128)S(1)} %slice.1082), channel_id=1, source_target_pairs={{16,0},{17,1},{18,2},{19,3},{20,4},{21,5},{22,6},{23,7},{24,8},{25... | collective-permute-start | bytes 24584 | tf_op jit(solution)/shard_map/ppermute | solution.py:46
  164.2 5.9 %collective-permute-start.7 = (f32[1,16,128]{2,1,0:T(8,128)S(1)}, f32[1,16,128]{2,1,0:T(8,128)S(1)}, u32[]{:S(2)}, u32[]{:S(2)}) collective-permute-start(f32[1,16,128]{2,1,0:T(8,128)S(1)} %slice.1082), channel_id=1, source_target_pairs={{0,16},{1,17},{2,18},{3,19},{4,20},{5,21},{6,22},{7,23},{8,24},{9,... | collective-permute-start | bytes 24584 | tf_op jit(solution)/shard_map/ppermute | solution.py:44
  170.1 5.9 %collective-permute-start.8 = (f32[10,1,128]{2,1,0:T(1,128)S(1)}, f32[10,1,128]{2,1,0:T(1,128)S(1)}, u32[]{:S(2)}, u32[]{:S(2)}) collective-permute-start(f32[10,1,128]{2,1,0:T(1,128)S(1)} %get-tuple-element.104), channel_id=1, source_target_pairs={{4,0},{8,4},{12,8},{5,1},{9,5},{13,9},{6,2},{10,6},{14,10},{7,3},{... | collective-permute-start | bytes 15368 | tf_op jit(solution)/shard_map/ppermute | solution.py:46
  171.4 5.9 %collective-permute-start.9 = (f32[10,1,128]{2,1,0:T(1,128)S(1)}, f32[10,1,128]{2,1,0:T(1,128)S(1)}, u32[]{:S(2)}, u32[]{:S(2)}) collective-permute-start(f32[10,1,128]{2,1,0:T(1,128)S(1)} %get-tuple-element.103), channel_id=1, source_target_pairs={{0,4},{4,8},{8,12},{1,5},{5,9},{9,13},{2,6},{6,10},{10,14},{3,7},{... | collective-permute-start | bytes 15368 | tf_op jit(solution)/shard_map/ppermute | solution.py:44
  177.4 4.4 %collective-permute-start.10 = (f32[10,18,1]{2,1,0:T(8,128)S(1)}, f32[10,18,1]{2,1,0:T(8,128)S(1)}, u32[]{:S(2)}, u32[]{:S(2)}) collective-permute-start(f32[10,18,1]{2,1,0:T(8,128)S(1)} %get-tuple-element.68), channel_id=1, source_target_pairs={{1,0},{2,1},{3,2},{5,4},{6,5},{7,6},{9,8},{10,9},{11,10},{13,12},{... | collective-permute-start | bytes 2168 | tf_op jit(solution)/shard_map/ppermute | solution.py:46
  178.7 4.0 collective-permute-start.11
  183.1 5.9 %collective-permute-start.12 = (f32[1,16,128]{2,1,0:T(8,128)S(1)}, f32[1,16,128]{2,1,0:T(8,128)S(1)}, u32[]{:S(2)}, u32[]{:S(2)}) collective-permute-start(f32[1,16,128]{2,1,0:T(8,128)S(1)} %get-tuple-element.110), channel_id=1, source_target_pairs={{16,0},{17,1},{18,2},{19,3},{20,4},{21,5},{22,6},{23,7},{24,8},{25... | collective-permute-start | bytes 24584 | tf_op jit(solution)/shard_map/ppermute | solution.py:46
  184.4 5.9 %collective-permute-start.13 = (f32[1,16,128]{2,1,0:T(8,128)S(1)}, f32[1,16,128]{2,1,0:T(8,128)S(1)}, u32[]{:S(2)}, u32[]{:S(2)}) collective-permute-start(f32[1,16,128]{2,1,0:T(8,128)S(1)} %get-tuple-element.109), channel_id=1, source_target_pairs={{0,16},{1,17},{2,18},{3,19},{4,20},{5,21},{6,22},{7,23},{8,24},{9,... | collective-permute-start | bytes 24584 | tf_op jit(solution)/shard_map/ppermute | solution.py:44
  190.3 6.1 %collective-permute-start.14 = (f32[10,1,128]{2,1,0:T(1,128)S(1)}, f32[10,1,128]{2,1,0:T(1,128)S(1)}, u32[]{:S(2)}, u32[]{:S(2)}) collective-permute-start(f32[10,1,128]{2,1,0:T(1,128)S(1)} %get-tuple-element.100), channel_id=1, source_target_pairs={{4,0},{8,4},{12,8},{5,1},{9,5},{13,9},{6,2},{10,6},{14,10},{7,3},{... | collective-permute-start | bytes 15368 | tf_op jit(solution)/shard_map/ppermute | solution.py:46
  191.6 6.1 %collective-permute-start.15 = (f32[10,1,128]{2,1,0:T(1,128)S(1)}, f32[10,1,128]{2,1,0:T(1,128)S(1)}, u32[]{:S(2)}, u32[]{:S(2)}) collective-permute-start(f32[10,1,128]{2,1,0:T(1,128)S(1)} %get-tuple-element.99), channel_id=1, source_target_pairs={{0,4},{4,8},{8,12},{1,5},{5,9},{9,13},{2,6},{6,10},{10,14},{3,7},{... | collective-permute-start | bytes 15368 | tf_op jit(solution)/shard_map/ppermute | solution.py:44
  197.9 4.6 %collective-permute-start.16 = (f32[10,18,1]{2,1,0:T(8,128)S(1)}, f32[10,18,1]{2,1,0:T(8,128)S(1)}, u32[]{:S(2)}, u32[]{:S(2)}) collective-permute-start(f32[10,18,1]{2,1,0:T(8,128)S(1)} %get-tuple-element.66), channel_id=1, source_target_pairs={{1,0},{2,1},{3,2},{5,4},{6,5},{7,6},{9,8},{10,9},{11,10},{13,12},{... | collective-permute-start | bytes 2168 | tf_op jit(solution)/shard_map/ppermute | solution.py:46
  199.2 4.0 collective-permute-start.17
  253.1 5.8 %collective-permute-start.18 = (f32[1,16,128]{2,1,0:T(8,128)S(1)}, f32[1,16,128]{2,1,0:T(8,128)S(1)}, u32[]{:S(2)}, u32[]{:S(2)}) collective-permute-start(f32[1,16,128]{2,1,0:T(8,128)S(1)} %slice.1129), channel_id=1, source_target_pairs={{16,0},{17,1},{18,2},{19,3},{20,4},{21,5},{22,6},{23,7},{24,8},{25... | collective-permute-start | bytes 24584 | tf_op jit(solution)/shard_map/ppermute | solution.py:46
  254.4 5.9 %collective-permute-start.19 = (f32[1,16,128]{2,1,0:T(8,128)S(1)}, f32[1,16,128]{2,1,0:T(8,128)S(1)}, u32[]{:S(2)}, u32[]{:S(2)}) collective-permute-start(f32[1,16,128]{2,1,0:T(8,128)S(1)} %slice.1129), channel_id=1, source_target_pairs={{0,16},{1,17},{2,18},{3,19},{4,20},{5,21},{6,22},{7,23},{8,24},{9,... | collective-permute-start | bytes 24584 | tf_op jit(solution)/shard_map/ppermute | solution.py:44
  260.3 7.8 %collective-permute-start.20 = (f32[10,1,128]{2,1,0:T(1,128)S(1)}, f32[10,1,128]{2,1,0:T(1,128)S(1)}, u32[]{:S(2)}, u32[]{:S(2)}) collective-permute-start(f32[10,1,128]{2,1,0:T(1,128)S(1)} %get-tuple-element.96), channel_id=1, source_target_pairs={{4,0},{8,4},{12,8},{5,1},{9,5},{13,9},{6,2},{10,6},{14,10},{7,3},{... | collective-permute-start | bytes 15368 | tf_op jit(solution)/shard_map/ppermute | solution.py:46
  261.6 6.5 %collective-permute-start.21 = (f32[10,1,128]{2,1,0:T(1,128)S(1)}, f32[10,1,128]{2,1,0:T(1,128)S(1)}, u32[]{:S(2)}, u32[]{:S(2)}) collective-permute-start(f32[10,1,128]{2,1,0:T(1,128)S(1)} %get-tuple-element.95), channel_id=1, source_target_pairs={{0,4},{4,8},{8,12},{1,5},{5,9},{9,13},{2,6},{6,10},{10,14},{3,7},{... | collective-permute-start | bytes 15368 | tf_op jit(solution)/shard_map/ppermute | solution.py:44
  268.3 4.4 %collective-permute-start.22 = (f32[10,18,1]{2,1,0:T(8,128)S(1)}, f32[10,18,1]{2,1,0:T(8,128)S(1)}, u32[]{:S(2)}, u32[]{:S(2)}) collective-permute-start(f32[10,18,1]{2,1,0:T(8,128)S(1)} %get-tuple-element.64), channel_id=1, source_target_pairs={{1,0},{2,1},{3,2},{5,4},{6,5},{7,6},{9,8},{10,9},{11,10},{13,12},{... | collective-permute-start | bytes 2168 | tf_op jit(solution)/shard_map/ppermute | solution.py:46
  269.6 4.0 collective-permute-start.23
  274.0 5.9 %collective-permute-start.24 = (f32[1,16,128]{2,1,0:T(8,128)S(1)}, f32[1,16,128]{2,1,0:T(8,128)S(1)}, u32[]{:S(2)}, u32[]{:S(2)}) collective-permute-start(f32[1,16,128]{2,1,0:T(8,128)S(1)} %get-tuple-element.108), channel_id=1, source_target_pairs={{16,0},{17,1},{18,2},{19,3},{20,4},{21,5},{22,6},{23,7},{24,8},{25... | collective-permute-start | bytes 24584 | tf_op jit(solution)/shard_map/ppermute | solution.py:46
  275.3 5.9 %collective-permute-start.25 = (f32[1,16,128]{2,1,0:T(8,128)S(1)}, f32[1,16,128]{2,1,0:T(8,128)S(1)}, u32[]{:S(2)}, u32[]{:S(2)}) collective-permute-start(f32[1,16,128]{2,1,0:T(8,128)S(1)} %get-tuple-element.107), channel_id=1, source_target_pairs={{0,16},{1,17},{2,18},{3,19},{4,20},{5,21},{6,22},{7,23},{8,24},{9,... | collective-permute-start | bytes 24584 | tf_op jit(solution)/shard_map/ppermute | solution.py:44
  281.2 5.9 %collective-permute-start.26 = (f32[10,1,128]{2,1,0:T(1,128)S(1)}, f32[10,1,128]{2,1,0:T(1,128)S(1)}, u32[]{:S(2)}, u32[]{:S(2)}) collective-permute-start(f32[10,1,128]{2,1,0:T(1,128)S(1)} %get-tuple-element.92), channel_id=1, source_target_pairs={{4,0},{8,4},{12,8},{5,1},{9,5},{13,9},{6,2},{10,6},{14,10},{7,3},{... | collective-permute-start | bytes 15368 | tf_op jit(solution)/shard_map/ppermute | solution.py:46
  282.5 5.9 %collective-permute-start.27 = (f32[10,1,128]{2,1,0:T(1,128)S(1)}, f32[10,1,128]{2,1,0:T(1,128)S(1)}, u32[]{:S(2)}, u32[]{:S(2)}) collective-permute-start(f32[10,1,128]{2,1,0:T(1,128)S(1)} %get-tuple-element.91), channel_id=1, source_target_pairs={{0,4},{4,8},{8,12},{1,5},{5,9},{9,13},{2,6},{6,10},{10,14},{3,7},{... | collective-permute-start | bytes 15368 | tf_op jit(solution)/shard_map/ppermute | solution.py:44
  288.5 4.6 %collective-permute-start.28 = (f32[10,18,1]{2,1,0:T(8,128)S(1)}, f32[10,18,1]{2,1,0:T(8,128)S(1)}, u32[]{:S(2)}, u32[]{:S(2)}) collective-permute-start(f32[10,18,1]{2,1,0:T(8,128)S(1)} %get-tuple-element.62), channel_id=1, source_target_pairs={{1,0},{2,1},{3,2},{5,4},{6,5},{7,6},{9,8},{10,9},{11,10},{13,12},{... | collective-permute-start | bytes 2168 | tf_op jit(solution)/shard_map/ppermute | solution.py:46
  289.8 4.2 collective-permute-start.29
  345.4 16.3 %collective-permute-start.36 = (f32[1,16,128]{2,1,0:T(8,128)S(1)}, f32[1,16,128]{2,1,0:T(8,128)S(1)}, u32[]{:S(2)}, u32[]{:S(2)}) collective-permute-start(f32[1,16,128]{2,1,0:T(8,128)S(1)} %slice.1200), channel_id=1, source_target_pairs={{16,0},{17,1},{18,2},{19,3},{20,4},{21,5},{22,6},{23,7},{24,8},{25... | collective-permute-start | bytes 24584 | tf_op jit(solution)/shard_map/ppermute | solution.py:46
  346.7 15.0 %collective-permute-start.37 = (f32[1,16,128]{2,1,0:T(8,128)S(1)}, f32[1,16,128]{2,1,0:T(8,128)S(1)}, u32[]{:S(2)}, u32[]{:S(2)}) collective-permute-start(f32[1,16,128]{2,1,0:T(8,128)S(1)} %slice.1200), channel_id=1, source_target_pairs={{0,16},{1,17},{2,18},{3,19},{4,20},{5,21},{6,22},{7,23},{8,24},{9,... | collective-permute-start | bytes 24584 | tf_op jit(solution)/shard_map/ppermute | solution.py:44
  355.8 11.8 %collective-permute-start.30 = (f32[1,16,128]{2,1,0:T(8,128)S(1)}, f32[1,16,128]{2,1,0:T(8,128)S(1)}, u32[]{:S(2)}, u32[]{:S(2)}) collective-permute-start(f32[1,16,128]{2,1,0:T(8,128)S(1)} %get-tuple-element.106), channel_id=1, source_target_pairs={{16,0},{17,1},{18,2},{19,3},{20,4},{21,5},{22,6},{23,7},{24,8},{25... | collective-permute-start | bytes 24584 | tf_op jit(solution)/shard_map/ppermute | solution.py:46
  357.1 10.5 %collective-permute-start.31 = (f32[1,16,128]{2,1,0:T(8,128)S(1)}, f32[1,16,128]{2,1,0:T(8,128)S(1)}, u32[]{:S(2)}, u32[]{:S(2)}) collective-permute-start(f32[1,16,128]{2,1,0:T(8,128)S(1)} %get-tuple-element.105), channel_id=1, source_target_pairs={{0,16},{1,17},{2,18},{3,19},{4,20},{5,21},{6,22},{7,23},{8,24},{9,... | collective-permute-start | bytes 24584 | tf_op jit(solution)/shard_map/ppermute | solution.py:44
  361.7 11.8 %collective-permute-start.38 = (f32[10,1,128]{2,1,0:T(1,128)S(1)}, f32[10,1,128]{2,1,0:T(1,128)S(1)}, u32[]{:S(2)}, u32[]{:S(2)}) collective-permute-start(f32[10,1,128]{2,1,0:T(1,128)S(1)} %get-tuple-element.84), channel_id=1, source_target_pairs={{4,0},{8,4},{12,8},{5,1},{9,5},{13,9},{6,2},{10,6},{14,10},{7,3},{... | collective-permute-start | bytes 15368 | tf_op jit(solution)/shard_map/ppermute | solution.py:46
  363.0 10.5 %collective-permute-start.39 = (f32[10,1,128]{2,1,0:T(1,128)S(1)}, f32[10,1,128]{2,1,0:T(1,128)S(1)}, u32[]{:S(2)}, u32[]{:S(2)}) collective-permute-start(f32[10,1,128]{2,1,0:T(1,128)S(1)} %get-tuple-element.83), channel_id=1, source_target_pairs={{0,4},{4,8},{8,12},{1,5},{5,9},{9,13},{2,6},{6,10},{10,14},{3,7},{... | collective-permute-start | bytes 15368 | tf_op jit(solution)/shard_map/ppermute | solution.py:44
  367.6 10.3 %collective-permute-start.32 = (f32[10,1,128]{2,1,0:T(1,128)S(1)}, f32[10,1,128]{2,1,0:T(1,128)S(1)}, u32[]{:S(2)}, u32[]{:S(2)}) collective-permute-start(f32[10,1,128]{2,1,0:T(1,128)S(1)} %get-tuple-element.88), channel_id=1, source_target_pairs={{4,0},{8,4},{12,8},{5,1},{9,5},{13,9},{6,2},{10,6},{14,10},{7,3},{... | collective-permute-start | bytes 15368 | tf_op jit(solution)/shard_map/ppermute | solution.py:46
  368.9 9.1 %collective-permute-start.33 = (f32[10,1,128]{2,1,0:T(1,128)S(1)}, f32[10,1,128]{2,1,0:T(1,128)S(1)}, u32[]{:S(2)}, u32[]{:S(2)}) collective-permute-start(f32[10,1,128]{2,1,0:T(1,128)S(1)} %get-tuple-element.87), channel_id=1, source_target_pairs={{0,4},{4,8},{8,12},{1,5},{5,9},{9,13},{2,6},{6,10},{10,14},{3,7},{... | collective-permute-start | bytes 15368 | tf_op jit(solution)/shard_map/ppermute | solution.py:44
  373.6 54.2 %collective-permute-start.40 = (f32[10,18,1]{2,1,0:T(8,128)S(1)}, f32[10,18,1]{2,1,0:T(8,128)S(1)}, u32[]{:S(2)}, u32[]{:S(2)}) collective-permute-start(f32[10,18,1]{2,1,0:T(8,128)S(1)} %get-tuple-element.58), channel_id=1, source_target_pairs={{1,0},{2,1},{3,2},{5,4},{6,5},{7,6},{9,8},{10,9},{11,10},{13,12},{... | collective-permute-start | bytes 2168 | tf_op jit(solution)/shard_map/ppermute | solution.py:46
  374.9 52.9 %collective-permute-start.41 = (f32[10,18,1]{2,1,0:T(8,128)S(1)}, f32[10,18,1]{2,1,0:T(8,128)S(1)}, u32[]{:S(2)}, u32[]{:S(2)}) collective-permute-start(f32[10,18,1]{2,1,0:T(8,128)S(1)} %get-tuple-element.57), channel_id=1, source_target_pairs={{0,1},{1,2},{2,3},{4,5},{5,6},{6,7},{8,9},{9,10},{10,11},{12,13},{... | collective-permute-start | bytes 2168 | tf_op jit(solution)/shard_map/ppermute | solution.py:44
  378.1 6.0 %collective-permute-start.34 = (f32[10,18,1]{2,1,0:T(8,128)S(1)}, f32[10,18,1]{2,1,0:T(8,128)S(1)}, u32[]{:S(2)}, u32[]{:S(2)}) collective-permute-start(f32[10,18,1]{2,1,0:T(8,128)S(1)} %get-tuple-element.60), channel_id=1, source_target_pairs={{1,0},{2,1},{3,2},{5,4},{6,5},{7,6},{9,8},{10,9},{11,10},{13,12},{... | collective-permute-start | bytes 2168 | tf_op jit(solution)/shard_map/ppermute | solution.py:46
  379.4 5.6 %collective-permute-start.35 = (f32[10,18,1]{2,1,0:T(8,128)S(1)}, f32[10,18,1]{2,1,0:T(8,128)S(1)}, u32[]{:S(2)}, u32[]{:S(2)}) collective-permute-start(f32[10,18,1]{2,1,0:T(8,128)S(1)} %get-tuple-element.59), channel_id=1, source_target_pairs={{0,1},{1,2},{2,3},{4,5},{5,6},{6,7},{8,9},{9,10},{10,11},{12,13},{... | collective-permute-start | bytes 2168 | tf_op jit(solution)/shard_map/ppermute | solution.py:44
